TPU v7x, 32 devices: a whole 2x2x4 slice. The times are simulated.
32 devices in a mesh: row: 8 (over y, x, core), col: 4 (over z).
Axes of the slice: x: 2, y: 2, z: 4, core: 2. Of those that a mesh axis runs over, the one named last changes fastest.
Arguments:
- sources: float32 [8, 4, 512, 512], P('row', 'col'), may hold values from -6 to 6
- leaf_basis: float32 [8, 4, 512, 256], P('row', 'col'), may hold values from -0.25 to 0.25
- transfers: float32 [8, 4, 4, 256, 512], P('row', 'col'), may hold values from -0.25 to 0.25
- out_basis: float32 [8, 4, 512, 256], P('row', 'col'), may hold values from -0.375 to 0.375
Outputs:
- result: float32 [8, 4, 512, 512], P('row', 'col')
All inputs are finite; a program needn't handle non-finite values.
Results may differ from a plain program's by a relative error of at most 0.0001.
Values sent between devices are 32-bit elements; how exact they have to be, the bound alone decides.
A program may use at most 64 MiB of HBM per device.

v0:
```python
import jax
import jax.numpy as jnp
from jax import lax
from jax.sharding import PartitionSpec as P


def swapped(x, axis, apart):
    return lax.ppermute(x, axis, [(i, i ^ 1 << apart) for i in range(lax.axis_size(axis))])


def mix_level(block, coeff, other):
    high = lax.Precision.HIGHEST
    width = coeff.shape[0]
    own = jnp.dot(block[:, :width], coeff, precision=high, preferred_element_type=jnp.float32)
    return own + jnp.dot(
        block[:, width:], other, precision=high, preferred_element_type=jnp.float32
    )


def body(sources, leaf_basis, transfers, out_basis):
    high = lax.Precision.HIGHEST
    levels = transfers.shape[2]
    row_bits = lax.axis_size("row").bit_length() - 1
    col_bits = lax.axis_size("col").bit_length() - 1
    coeff = jnp.einsum("mk,mr->kr", leaf_basis[0, 0], sources[0, 0], precision=high)
    half = coeff.shape[1] // 2
    groups = [coeff[:, :half], coeff[:, half:]]
    for level in range(levels):
        fresh = []
        for member in groups:
            if level % 2 == 0:
                other = swapped(member, "row", row_bits - 1 - level // 2)
            else:
                other = swapped(member, "col", col_bits - 1 - level // 2)
            fresh.append(mix_level(transfers[0, 0, level], member, other))
        groups = fresh
    coeff = jnp.concatenate(groups, axis=1)
    result = jnp.dot(out_basis[0, 0], coeff, precision=high, preferred_element_type=jnp.float32)
    return result[None, None]


def solution(mesh):
    in_specs = (
        P("row", "col", None, None),
        P("row", "col", None, None),
        P("row", "col", None, None, None),
        P("row", "col", None, None),
    )
    out_specs = P("row", "col", None, None)
    return jax.shard_map(body, mesh=mesh, in_specs=in_specs, out_specs=out_specs, check_vma=False)
```

profile of v0, /device:TPU:0, one launch (start us, length us, event | category | flops | bytes accessed | tf_op | source)
XLA Modules:
  0.0 63.3 jit_solution(7840227245495337697)
XLA Ops:
  0.0 0.0 copy-start
  0.0 0.0 copy-start.1
  0.0 1.2 %copy-done = f32[1,1,512,512]{3,2,1,0:T(8,128)S(1)} copy-done((f32[1,1,512,512]{3,2,1,0:T(8,128)S(1)}, f32[1,1,512,512]{3,2,1,0:T(8,128)}, u32[]{:S(2)}) %copy-start) | copy-done | bytes 1048600
  1.2 2.1 %fusion.2 = f32[256,512]{1,0:T(8,128)S(1)} fusion(f32[1,1,512,512]{3,2,1,0:T(8,128)S(1)} %copy-done, f32[1,1,512,256]{3,2,1,0:T(8,128)} %param.5), kind=kOutput, calls=%fused_computation.11 | convolution fusion | flops 805306368 | bytes 2097152 | tf_op jit(solution)/shard_map/mk,mr->kr/dot_general | solution.py:25
  3.4 3.1 %collective-permute-start = (f32[256,256]{1,0:T(8,128)S(1)}, f32[256,256]{1,0:T(8,128)S(1)}, u32[]{:S(2)}, u32[]{:S(2)}) collective-permute-start(f32[256,256]{1,0:T(8,128)S(1)} %get-tuple-element.9), channel_id=1, source_target_pairs={{0,16},{4,20},{8,24},{12,28},{16,0},{20,4},{24,8},{28,12},{1,17},{... | collective-permute-start | bytes 786440 | tf_op jit(solution)/shard_map/ppermute | solution.py:8
  6.4 0.1 collective-permute-start.4
  6.5 0.0 copy-done.1
  6.5 0.2 slice_bitcast_fusion
  6.7 0.6 fusion.29
  7.3 0.6 fusion.31
  7.9 10.5 %collective-permute-done.4 = f32[256,256]{1,0:T(8,128)S(1)} collective-permute-done((f32[256,256]{1,0:T(8,128)S(1)}, f32[256,256]{1,0:T(8,128)S(1)}, u32[]{:S(2)}, u32[]{:S(2)}) %collective-permute-start.4) | collective-permute-done | bytes 262176 | tf_op jit(solution)/shard_map/ppermute | solution.py:8
  18.4 0.6 convolution_add_fusion.3
  19.0 2.9 %collective-permute-start.5 = (f32[256,256]{0,1:T(8,128)S(1)}, f32[256,256]{0,1:T(8,128)S(1)}, u32[]{:S(2)}, u32[]{:S(2)}) collective-permute-start(f32[256,256]{0,1:T(8,128)S(1)} %bitcast.46), channel_id=1, source_target_pairs={{0,2},{1,3},{2,0},{3,1},{4,6},{5,7},{6,4},{7,5},{8,10},{9,11},{10,... | collective-permute-start | bytes 786440 | tf_op jit(solution)/shard_map/ppermute | solution.py:8
  21.8 0.0 collective-permute-done
  21.8 0.6 convolution_add_fusion.7
  22.4 0.4 fusion.25
  22.9 0.2 collective-permute-start.1
  23.0 0.4 fusion.23
  23.5 16.2 %collective-permute-done.5 = f32[256,256]{0,1:T(8,128)S(1)} collective-permute-done((f32[256,256]{0,1:T(8,128)S(1)}, f32[256,256]{0,1:T(8,128)S(1)}, u32[]{:S(2)}, u32[]{:S(2)}) %collective-permute-start.5) | collective-permute-done | bytes 262176 | tf_op jit(solution)/shard_map/ppermute | solution.py:8
  39.7 0.4 convolution_add_fusion.2
  40.1 1.6 %collective-permute-start.6 = (f32[256,256]{0,1:T(8,128)S(1)}, f32[256,256]{0,1:T(8,128)S(1)}, u32[]{:S(2)}, u32[]{:S(2)}) collective-permute-start(f32[256,256]{0,1:T(8,128)S(1)} %bitcast.48), channel_id=1, source_target_pairs={{0,8},{4,12},{8,0},{12,4},{16,24},{20,28},{24,16},{28,20},{1,9},{5... | collective-permute-start | bytes 786440 | tf_op jit(solution)/shard_map/ppermute | solution.py:8
  41.7 2.6 %collective-permute-done.1 = f32[256,256]{0,1:T(8,128)S(1)} collective-permute-done((f32[256,256]{0,1:T(8,128)S(1)}, f32[256,256]{0,1:T(8,128)S(1)}, u32[]{:S(2)}, u32[]{:S(2)}) %collective-permute-start.1) | collective-permute-done | bytes 262176 | tf_op jit(solution)/shard_map/ppermute | solution.py:8
  44.3 0.4 convolution_add_fusion.6
  44.7 0.4 fusion.17
  45.1 1.5 %collective-permute-start.2 = (f32[256,256]{0,1:T(8,128)S(1)}, f32[256,256]{0,1:T(8,128)S(1)}, u32[]{:S(2)}, u32[]{:S(2)}) collective-permute-start(f32[256,256]{0,1:T(8,128)S(1)} %bitcast.49), channel_id=1, source_target_pairs={{0,8},{4,12},{8,0},{12,4},{16,24},{20,28},{24,16},{28,20},{1,9},{5... | collective-permute-start | bytes 786440 | tf_op jit(solution)/shard_map/ppermute | solution.py:8
  46.6 0.4 fusion.19
  47.0 0.0 collective-permute-done.6
  47.0 0.4 convolution_add_fusion.1
  47.4 1.0 %collective-permute-start.7 = (f32[256,256]{0,1:T(8,128)S(1)}, f32[256,256]{0,1:T(8,128)S(1)}, u32[]{:S(2)}, u32[]{:S(2)}) collective-permute-start(f32[256,256]{0,1:T(8,128)S(1)} %bitcast.45), channel_id=1, source_target_pairs={{0,1},{1,0},{2,3},{3,2},{4,5},{5,4},{6,7},{7,6},{8,9},{9,8},{10,11... | collective-permute-start | bytes 786440 | tf_op jit(solution)/shard_map/ppermute | solution.py:8
  48.4 4.0 %collective-permute-done.2 = f32[256,256]{0,1:T(8,128)S(1)} collective-permute-done((f32[256,256]{0,1:T(8,128)S(1)}, f32[256,256]{0,1:T(8,128)S(1)}, u32[]{:S(2)}, u32[]{:S(2)}) %collective-permute-start.2) | collective-permute-done | bytes 262176 | tf_op jit(solution)/shard_map/ppermute | solution.py:8
  52.4 0.4 convolution_add_fusion.5
  52.9 0.0 copy-start.2
  52.9 0.4 fusion.11
  53.3 1.6 %collective-permute-start.3 = (f32[256,256]{0,1:T(8,128)S(1)}, f32[256,256]{0,1:T(8,128)S(1)}, u32[]{:S(2)}, u32[]{:S(2)}) collective-permute-start(f32[256,256]{0,1:T(8,128)S(1)} %bitcast.50), channel_id=1, source_target_pairs={{0,1},{1,0},{2,3},{3,2},{4,5},{5,4},{6,7},{7,6},{8,9},{9,8},{10,11... | collective-permute-start | bytes 786440 | tf_op jit(solution)/shard_map/ppermute | solution.py:8
  54.9 0.4 fusion.13
  55.3 0.0 collective-permute-done.7
  55.3 0.4 fusion
  55.8 4.8 %collective-permute-done.3 = f32[256,256]{0,1:T(8,128)S(1)} collective-permute-done((f32[256,256]{0,1:T(8,128)S(1)}, f32[256,256]{0,1:T(8,128)S(1)}, u32[]{:S(2)}, u32[]{:S(2)}) %collective-permute-start.3) | collective-permute-done | bytes 262176 | tf_op jit(solution)/shard_map/ppermute | solution.py:8
  60.6 0.4 fusion.1
  61.0 0.0 copy-done.2
  61.0 1.0 %convolution_bitcast_fusion = f32[1,1,512,512]{2,3,1,0:T(8,128)S(1)} fusion(f32[256,256]{0,1:T(8,128)S(1)} %fusion, f32[256,256]{0,1:T(8,128)S(1)} %fusion.1, f32[1,1,512,256]{3,2,1,0:T(8,128)S(1)} %copy-done.2), kind=kOutput, calls=%fused_computation | convolution fusion | flops 805437440 | bytes 2097152 | tf_op jit(solution)/shard_map/dot_general | solution.py:38
  62.0 1.3 %copy.5 = f32[1,1,512,512]{3,2,1,0:T(8,128)} copy(f32[1,1,512,512]{2,3,1,0:T(8,128)S(1)} %convolution_bitcast_fusion) | data formatting | bytes 2097152 | tf_op jit(solution)/shard_map/broadcast_in_dim | solution.py:39
  (1 shorter events, 0.0 us)
Async XLA Ops:
  0.0 1.2 %copy-start = (f32[1,1,512,512]{3,2,1,0:T(8,128)S(1)}, f32[1,1,512,512]{3,2,1,0:T(8,128)}, u32[]{:S(2)}) copy-start(f32[1,1,512,512]{3,2,1,0:T(8,128)} %param.4) | copy-start | bytes 3145732
  0.0 6.5 %copy-start.1 = (f32[1,1,4,256,512]{4,3,2,1,0:T(8,128)S(1)}, f32[1,1,4,256,512]{4,3,2,1,0:T(8,128)}, u32[]{:S(2)}) copy-start(f32[1,1,4,256,512]{4,3,2,1,0:T(8,128)} %param.6) | copy-start | bytes 6291460
  3.4 18.5 %collective-permute-start = (f32[256,256]{1,0:T(8,128)S(1)}, f32[256,256]{1,0:T(8,128)S(1)}, u32[]{:S(2)}, u32[]{:S(2)}) collective-permute-start(f32[256,256]{1,0:T(8,128)S(1)} %get-tuple-element.9), channel_id=1, source_target_pairs={{0,16},{4,20},{8,24},{12,28},{16,0},{20,4},{24,8},{28,12},{1,17},{... | collective-permute-start | bytes 786440 | tf_op jit(solution)/shard_map/ppermute | solution.py:8
  6.4 11.9 %collective-permute-start.4 = (f32[256,256]{1,0:T(8,128)S(1)}, f32[256,256]{1,0:T(8,128)S(1)}, u32[]{:S(2)}, u32[]{:S(2)}) collective-permute-start(f32[256,256]{1,0:T(8,128)S(1)} %get-tuple-element.10), channel_id=1, source_target_pairs={{0,16},{4,20},{8,24},{12,28},{16,0},{20,4},{24,8},{28,12},{1,17},{... | collective-permute-start | bytes 786440 | tf_op jit(solution)/shard_map/ppermute | solution.py:8
  19.0 20.7 %collective-permute-start.5 = (f32[256,256]{0,1:T(8,128)S(1)}, f32[256,256]{0,1:T(8,128)S(1)}, u32[]{:S(2)}, u32[]{:S(2)}) collective-permute-start(f32[256,256]{0,1:T(8,128)S(1)} %bitcast.46), channel_id=1, source_target_pairs={{0,2},{1,3},{2,0},{3,1},{4,6},{5,7},{6,4},{7,5},{8,10},{9,11},{10,... | collective-permute-start | bytes 786440 | tf_op jit(solution)/shard_map/ppermute | solution.py:8
  22.9 21.4 %collective-permute-start.1 = (f32[256,256]{0,1:T(8,128)S(1)}, f32[256,256]{0,1:T(8,128)S(1)}, u32[]{:S(2)}, u32[]{:S(2)}) collective-permute-start(f32[256,256]{0,1:T(8,128)S(1)} %bitcast.47), channel_id=1, source_target_pairs={{0,2},{1,3},{2,0},{3,1},{4,6},{5,7},{6,4},{7,5},{8,10},{9,11},{10,... | collective-permute-start | bytes 786440 | tf_op jit(solution)/shard_map/ppermute | solution.py:8
  40.1 6.9 %collective-permute-start.6 = (f32[256,256]{0,1:T(8,128)S(1)}, f32[256,256]{0,1:T(8,128)S(1)}, u32[]{:S(2)}, u32[]{:S(2)}) collective-permute-start(f32[256,256]{0,1:T(8,128)S(1)} %bitcast.48), channel_id=1, source_target_pairs={{0,8},{4,12},{8,0},{12,4},{16,24},{20,28},{24,16},{28,20},{1,9},{5... | collective-permute-start | bytes 786440 | tf_op jit(solution)/shard_map/ppermute | solution.py:8
  45.1 7.3 %collective-permute-start.2 = (f32[256,256]{0,1:T(8,128)S(1)}, f32[256,256]{0,1:T(8,128)S(1)}, u32[]{:S(2)}, u32[]{:S(2)}) collective-permute-start(f32[256,256]{0,1:T(8,128)S(1)} %bitcast.49), channel_id=1, source_target_pairs={{0,8},{4,12},{8,0},{12,4},{16,24},{20,28},{24,16},{28,20},{1,9},{5... | collective-permute-start | bytes 786440 | tf_op jit(solution)/shard_map/ppermute | solution.py:8
  47.4 7.9 %collective-permute-start.7 = (f32[256,256]{0,1:T(8,128)S(1)}, f32[256,256]{0,1:T(8,128)S(1)}, u32[]{:S(2)}, u32[]{:S(2)}) collective-permute-start(f32[256,256]{0,1:T(8,128)S(1)} %bitcast.45), channel_id=1, source_target_pairs={{0,1},{1,0},{2,3},{3,2},{4,5},{5,4},{6,7},{7,6},{8,9},{9,8},{10,11... | collective-permute-start | bytes 786440 | tf_op jit(solution)/shard_map/ppermute | solution.py:8
  52.9 8.1 %copy-start.2 = (f32[1,1,512,256]{3,2,1,0:T(8,128)S(1)}, f32[1,1,512,256]{3,2,1,0:T(8,128)}, u32[]{:S(2)}) copy-start(f32[1,1,512,256]{3,2,1,0:T(8,128)} %param.7) | copy-start | bytes 1572868
  53.3 7.3 %collective-permute-start.3 = (f32[256,256]{0,1:T(8,128)S(1)}, f32[256,256]{0,1:T(8,128)S(1)}, u32[]{:S(2)}, u32[]{:S(2)}) collective-permute-start(f32[256,256]{0,1:T(8,128)S(1)} %bitcast.50), channel_id=1, source_target_pairs={{0,1},{1,0},{2,3},{3,2},{4,5},{5,4},{6,7},{7,6},{8,9},{9,8},{10,11... | collective-permute-start | bytes 786440 | tf_op jit(solution)/shard_map/ppermute | solution.py:8
where the time goes:
time: 63.5 us; the launch traced here: 63.3 us
  waiting for transfers between devices  38 us (60%)
  starting transfers between devices  11.9 us (19%)
  matrix products  10.4 us (16%)
  local copies, waits for them, and re-layouts  2.75 us (4%)
    ppermute x8, waiting for transfers between devices, swapped(): lax.ppermute(x, axis, [(i, i ^ 1 << apart) for i in range(lax.axis_size(a...  38 us
    ppermute x8, starting transfers between devices, swapped(): lax.ppermute(x, axis, [(i, i ^ 1 << apart) for i in range(lax.axis_size(a...  11.9 us
    dot_general x8, matrix products, mix_level(): jnp.dot(block[:, width:], other, precision=high, preferred_element_type=j...  3.67 us
    dot_general x8, matrix products, mix_level(): jnp.dot(block[:, :width], coeff, precision=high, preferred_element_type=j...  3.65 us
    dot_general x1, matrix products, body(): jnp.einsum('mk,mr->kr', leaf_basis[0, 0], sources[0, 0], precision=high)  2.1 us
    broadcast_in_dim x1, local copies, waits for them, and re-layouts, body(): return result[None, None]  1.31 us
  transfers between devices with their start and end apart: 8, of which 5 were waited for; matrix products, arithmetic and copies ran while one was open for 11% of the time, Pallas kernels for 0%

commit v1 on v0

v1 whole, which is shorter than its diff:
```python
import functools

import jax
import jax.numpy as jnp
from jax import lax
from jax.experimental import pallas as pl
from jax.experimental.pallas import tpu as pltpu
from jax.sharding import PartitionSpec as P

GROUP = 128
CHUNK = 64


def split(x):
    high = x.astype(jnp.bfloat16)
    return high, (x - high.astype(jnp.float32)).astype(jnp.bfloat16)


def product(left, right_high, right_low, right_dim):
    dims = (((1,), (right_dim,)), ((), ()))
    rows = left.shape[0]
    high, low = split(left)
    both = lax.dot_general(
        jnp.concatenate([high, low], axis=0), right_high, dims, preferred_element_type=jnp.float32
    )
    rest = lax.dot_general(high, right_low, dims, preferred_element_type=jnp.float32)
    return both[:rows] + (both[rows:] + rest)


def order_of(count, levels):
    unit = 8.0 / count
    steps = []
    for at in range(count):
        ready = 3.4 + 2.8 * unit * at
        for level in range(levels):
            steps.append((ready, -level, at, level))
            ready += (3.5 + 1.4 * unit) if level % 2 == 0 else 3.5
    return [(at, level) for _, _, at, level in sorted(steps)]


def partner(level, levels):
    axis = "row" if level % 2 == 0 else "col"
    span = lax.axis_size(axis) >> (1 + level // 2)
    me = lax.axis_index(axis)
    return {axis: me + span - 2 * span * ((me // span) % 2)}


def kernel(
    src, leaf, tra, outb, res,
    src_v, leaf_v, tra_v, outb_v, res_v, coeff, other, t_high, t_low,
    in_sem, tra_sem, out_sem, send_sem, recv_sem,
):
    levels, rank = tra.shape[0], leaf.shape[1]
    rhs = src.shape[1]
    groups, count = rhs // GROUP, rhs // CHUNK
    partners = [partner(level, levels) for level in range(levels)]

    barrier = pltpu.get_barrier_semaphore()
    for who in partners:
        pl.semaphore_signal(barrier, inc=1, device_id=who, device_id_type=pl.DeviceIdType.MESH)

    load_leaf = pltpu.make_async_copy(leaf, leaf_v, in_sem.at[groups])
    load_leaf.start()
    load_src = []
    for g in range(groups):
        cols = pl.ds(g * GROUP, GROUP)
        load_src.append(pltpu.make_async_copy(src.at[:, cols], src_v.at[:, cols], in_sem.at[g]))
        load_src[-1].start()
    load_tra = [pltpu.make_async_copy(tra.at[k], tra_v.at[k], tra_sem.at[k]) for k in range(levels)]
    for copy in load_tra:
        copy.start()
    load_out = pltpu.make_async_copy(outb, outb_v, in_sem.at[groups + 1])
    load_out.start()

    copies = {}

    def send(at, level):
        rows = pl.ds(at * CHUNK, CHUNK)
        copy = pltpu.make_async_remote_copy(
            src_ref=coeff.at[level, rows],
            dst_ref=other.at[level, rows],
            send_sem=send_sem.at[level, at],
            recv_sem=recv_sem.at[level, at],
            device_id=partners[level],
            device_id_type=pl.DeviceIdType.MESH,
        )
        copy.start()
        copies[at, level] = copy

    load_leaf.wait()
    l_high, l_low = split(leaf_v[...])
    for g in range(groups):
        load_src[g].wait()
        turned = src_v[:, g * GROUP:(g + 1) * GROUP].T
        coeff[0, pl.ds(g * GROUP, GROUP), :] = product(turned, l_high, l_low, 0)
        if g == 0:
            pl.semaphore_wait(barrier, levels)
        for at in range(g * GROUP // CHUNK, (g + 1) * GROUP // CHUNK):
            send(at, 0)
    for k in range(levels):
        load_tra[k].wait()
        high, low = split(tra_v[k])
        t_high[k] = high
        t_low[k] = low
    load_out.wait()

    stores = []
    done = set()
    for at, level in order_of(count, levels):
        rows = pl.ds(at * CHUNK, CHUNK)
        own = product(coeff[level, rows, :], t_high[level, :, :rank], t_low[level, :, :rank], 1)
        copies[at, level].wait_recv()
        fresh = own + product(
            other[level, rows, :], t_high[level, :, rank:], t_low[level, :, rank:], 1
        )
        coeff[level + 1, rows, :] = fresh
        if level + 1 < levels:
            send(at, level + 1)
            continue
        done.add(at)
        g = at * CHUNK // GROUP
        if all(m in done for m in range(g * GROUP // CHUNK, (g + 1) * GROUP // CHUNK)):
            cols = pl.ds(g * GROUP, GROUP)
            last_high, last_low = split(coeff[levels, cols, :])
            res_v[:, g * GROUP:(g + 1) * GROUP] = product(outb_v[...], last_high, last_low, 1)
            stores.append(pltpu.make_async_copy(res_v.at[:, cols], res.at[:, cols], out_sem.at[g]))
            stores[-1].start()
    for copy in copies.values():
        copy.wait_send()
    for copy in stores:
        copy.wait()


def body(sources, leaf_basis, transfers, out_basis):
    src, leaf, tra, outb = sources[0, 0], leaf_basis[0, 0], transfers[0, 0], out_basis[0, 0]
    size, rhs = src.shape
    rank = leaf.shape[1]
    levels = tra.shape[0]
    f32 = jnp.float32
    any_space = pl.BlockSpec(memory_space=pl.ANY)
    result = pl.pallas_call(
        kernel,
        out_shape=jax.ShapeDtypeStruct((size, rhs), f32),
        in_specs=[any_space] * 4,
        out_specs=any_space,
        scratch_shapes=[
            pltpu.VMEM((size, rhs), f32),
            pltpu.VMEM((size, rank), f32),
            pltpu.VMEM(tra.shape, f32),
            pltpu.VMEM((size, rank), f32),
            pltpu.VMEM((size, rhs), f32),
            pltpu.VMEM((levels + 1, rhs, rank), f32),
            pltpu.VMEM((levels, rhs, rank), f32),
            pltpu.VMEM(tra.shape, jnp.bfloat16),
            pltpu.VMEM(tra.shape, jnp.bfloat16),
            pltpu.SemaphoreType.DMA((rhs // GROUP + 2,)),
            pltpu.SemaphoreType.DMA((levels,)),
            pltpu.SemaphoreType.DMA((rhs // GROUP,)),
            pltpu.SemaphoreType.DMA((levels, rhs // CHUNK)),
            pltpu.SemaphoreType.DMA((levels, rhs // CHUNK)),
        ],
        compiler_params=pltpu.CompilerParams(collective_id=0, has_side_effects=True),
    )(src, leaf, tra, outb)
    return result[None, None]


def solution(mesh):
    in_specs = (
        P("row", "col", None, None),
        P("row", "col", None, None),
        P("row", "col", None, None, None),
        P("row", "col", None, None),
    )
    out_specs = P("row", "col", None, None)
    return jax.shard_map(body, mesh=mesh, in_specs=in_specs, out_specs=out_specs, check_vma=False)
```

time: 63.5 us -> 48.2 us (0.76)
  Pallas kernels: 0 us -> 45.8 us
  waiting for transfers between devices: 38 us -> 0 us
  starting transfers between devices: 11.9 us -> 0 us
  matrix products: 10.4 us -> 0 us
    pallas_call x0 -> x1, Pallas kernels: none -> 45.8 us  [body(): pl.pallas_call(kernel, out_shape=jax.ShapeDtypeStruct((size, rhs), f32),...]
    ppermute x8 -> x0, waiting for transfers between devices: 38 us -> none  [swapped(): lax.ppermute(x, axis, [(i, i ^ 1 << apart) for i in range(lax.axis_size(a...]
    ppermute x8 -> x0, starting transfers between devices: 11.9 us -> none  [swapped(): lax.ppermute(x, axis, [(i, i ^ 1 << apart) for i in range(lax.axis_size(a...]
    dot_general x18 -> x0, matrix products: 10.4 us -> none  [the longest x8 3.67 us: mix_level(): jnp.dot(block[:, width:], other, precision=high, preferred_element_type=j...]
    broadcast_in_dim x1 -> x0, local copies, waits for them, and re-layouts: 1.31 us -> none  [body(): return result[None, None]]
    unnamed x6 -> x1, local copies, waits for them, and re-layouts: 1.23 us -> 2.26 us
  transfers between devices with their start and end apart: 8 -> 0, of which waited for: 5 -> 0; matrix products, arithmetic and copies ran while one was open for 11% -> 0% of each run, Pallas kernels for 0% -> 0%
where the time goes in v1:
time: 48.2 us; the launch traced here: 48.1 us
  Pallas kernels  45.8 us (95%)
  local copies, waits for them, and re-layouts  2.26 us (5%)
    pallas_call x1, Pallas kernels, body(): pl.pallas_call(kernel, out_shape=jax.ShapeDtypeStruct((size, rhs), f32),...  45.8 us
    unnamed x1, local copies, waits for them, and re-layouts  2.26 us

profile of v1, /device:TPU:0, one launch (start us, length us, event | category | flops | bytes accessed | tf_op | source)
XLA Modules:
  0.0 48.1 jit_solution(438331502526756237)
XLA Ops:
  0.0 45.8 %shard_map.46 = f32[512,512]{1,0:T(8,128)} custom-call(f32[512,512]{1,0:T(8,128)} %bitcast.7, f32[512,256]{1,0:T(8,128)} %bitcast.8, f32[4,256,512]{2,1,0:T(8,128)} %bitcast.6, f32[512,256]{1,0:T(8,128)} %bitcast.9), custom_call_target="tpu_custom_call" | custom-call | tf_op jit(solution)/shard_map/pallas_call | solution.py:141
  45.8 2.3 %copy.6 = f32[1,1,512,512]{3,2,1,0:T(8,128)} copy(f32[1,1,512,512]{3,2,1,0:T(8,128)} %bitcast.5) | data formatting | bytes 2097152

commit v2 on v1

v2 whole, which is shorter than its diff:
```python
import jax
import jax.numpy as jnp
from jax import lax
from jax.experimental import pallas as pl
from jax.experimental.pallas import tpu as pltpu
from jax.sharding import PartitionSpec as P

GROUP = 128
CHUNK = 64
LAGS = (320, 160)
RAMP = (32, 32, 64)
WIDE = 512


def split(x):
    high = x.astype(jnp.bfloat16)
    return high, (x - high.astype(jnp.float32)).astype(jnp.bfloat16)


def product(left, right_high, right_low, right_dim):
    dims = (((1,), (right_dim,)), ((), ()))
    rows = left.shape[0]
    high, low = split(left)
    both = lax.dot_general(
        jnp.concatenate([high, low], axis=0), right_high, dims, preferred_element_type=jnp.float32
    )
    rest = lax.dot_general(high, right_low, dims, preferred_element_type=jnp.float32)
    return both[:rows] + (both[rows:] + rest)


def chunks_of(rhs):
    body = rhs - 2 * sum(RAMP)
    sizes = list(RAMP) + [CHUNK] * (body // CHUNK)
    if body % CHUNK:
        sizes.append(body % CHUNK)
    sizes += list(RAMP)[::-1]
    starts = [sum(sizes[:at]) for at in range(len(sizes))]
    return list(zip(starts, sizes))


def order_of(chunks, levels):
    steps = []
    for at, (start, size) in enumerate(chunks):
        for level in range(levels):
            lag = LAGS[0] * ((level + 1) // 2) + LAGS[1] * (level // 2)
            steps.append((start + lag, -level, at, level))
    return [(at, -low) for _, low, at, _ in sorted(steps)]


def partner(level, levels):
    axis = "row" if level % 2 == 0 else "col"
    span = lax.axis_size(axis) >> (1 + level // 2)
    me = lax.axis_index(axis)
    return {axis: me + span - 2 * span * ((me // span) % 2)}


def kernel(
    src, leaf, tra, res,
    src_v, leaf_v, tra_v, coeff, other, t_high, t_low,
    in_sem, tra_sem, out_sem, send_sem, recv_sem,
):
    levels, rank = tra.shape[0], leaf.shape[1]
    rhs = src.shape[1]
    groups = rhs // GROUP
    chunks = chunks_of(rhs)
    partners = [partner(level, levels) for level in range(levels)]

    barrier = pltpu.get_barrier_semaphore()
    for who in partners:
        pl.semaphore_signal(barrier, inc=1, device_id=who, device_id_type=pl.DeviceIdType.MESH)

    load_leaf = pltpu.make_async_copy(leaf, leaf_v, in_sem.at[groups])
    load_leaf.start()
    load_src = []
    for g in range(groups):
        cols = pl.ds(g * GROUP, GROUP)
        load_src.append(pltpu.make_async_copy(src.at[:, cols], src_v.at[:, cols], in_sem.at[g]))
        load_src[-1].start()
    load_tra = [pltpu.make_async_copy(tra.at[k], tra_v.at[k], tra_sem.at[k]) for k in range(levels)]
    for copy in load_tra:
        copy.start()

    copies = {}

    def send(at, level):
        rows = pl.ds(*chunks[at])
        copy = pltpu.make_async_remote_copy(
            src_ref=coeff.at[level, rows],
            dst_ref=other.at[level, rows],
            send_sem=send_sem.at[level, at],
            recv_sem=recv_sem.at[level, at],
            device_id=partners[level],
            device_id_type=pl.DeviceIdType.MESH,
        )
        copy.start()
        copies[at, level] = copy

    load_leaf.wait()
    l_high, l_low = split(leaf_v[...])
    for g in range(groups):
        load_src[g].wait()
        turned = src_v[:, g * GROUP:(g + 1) * GROUP].T
        coeff[0, pl.ds(g * GROUP, GROUP), :] = product(turned, l_high, l_low, 0)
        if g == 0:
            pl.semaphore_wait(barrier, levels)
        for at, (start, size) in enumerate(chunks):
            if g * GROUP < start + size <= (g + 1) * GROUP:
                send(at, 0)
    def prepare(k):
        load_tra[k].wait()
        high, low = split(tra_v[k].T)
        t_high[k] = high
        t_low[k] = low

    def mix(k, left, half):
        part = slice(half * rank, (half + 1) * rank)
        return product(left, t_high[k, part, :], t_low[k, part, :], 0)

    prepared = 0

    stores = []
    for at, level in order_of(chunks, levels):
        rows = pl.ds(*chunks[at])
        if level == prepared:
            prepare(level)
            prepared += 1
        own = mix(level, coeff[level, rows, :], 0)
        copies[at, level].wait_recv()
        fresh = own + mix(level, other[level, rows, :], 1)
        coeff[level + 1, rows, :] = fresh
        if level + 1 < levels:
            send(at, level + 1)
            continue
        stores.append(pltpu.make_async_copy(coeff.at[levels, rows], res.at[rows], out_sem.at[at]))
        stores[-1].start()
    for copy in copies.values():
        copy.wait_send()
    for copy in stores:
        copy.wait()


def expand(last, outb, res):
    last_high, last_low = split(last[...])
    res[...] = product(outb[...], last_high, last_low, 1)


def body(sources, leaf_basis, transfers, out_basis):
    src, leaf, tra, outb = sources[0, 0], leaf_basis[0, 0], transfers[0, 0], out_basis[0, 0]
    size, rhs = src.shape
    rank = leaf.shape[1]
    count = len(chunks_of(rhs))
    levels = tra.shape[0]
    f32 = jnp.float32
    any_space = pl.BlockSpec(memory_space=pl.ANY)
    hbm = pl.BlockSpec(memory_space=pltpu.HBM)
    last = pl.pallas_call(
        kernel,
        out_shape=jax.ShapeDtypeStruct((rhs, rank), f32),
        in_specs=[hbm] * 3,
        out_specs=any_space,
        scratch_shapes=[
            pltpu.VMEM((size, rhs), f32),
            pltpu.VMEM((size, rank), f32),
            pltpu.VMEM(tra.shape, f32),
            pltpu.VMEM((levels + 1, rhs, rank), f32),
            pltpu.VMEM((levels, rhs, rank), f32),
            pltpu.VMEM((levels, 2 * rank, rank), jnp.bfloat16),
            pltpu.VMEM((levels, 2 * rank, rank), jnp.bfloat16),
            pltpu.SemaphoreType.DMA((rhs // GROUP + 1,)),
            pltpu.SemaphoreType.DMA((levels,)),
            pltpu.SemaphoreType.DMA((count,)),
            pltpu.SemaphoreType.DMA((levels, count)),
            pltpu.SemaphoreType.DMA((levels, count)),
        ],
        compiler_params=pltpu.CompilerParams(collective_id=0, has_side_effects=True),
    )(src, leaf, tra)
    wide = min(WIDE, rhs)
    result = pl.pallas_call(
        expand,
        grid=(rhs // wide,),
        out_shape=jax.ShapeDtypeStruct((size, rhs), f32),
        in_specs=[
            pl.BlockSpec((wide, rank), lambda i: (i, 0)),
            pl.BlockSpec((size, rank), lambda i: (0, 0)),
        ],
        out_specs=pl.BlockSpec((size, wide), lambda i: (0, i)),
    )(last, outb)
    return result[None, None]


def solution(mesh):
    in_specs = (
        P("row", "col", None, None),
        P("row", "col", None, None),
        P("row", "col", None, None, None),
        P("row", "col", None, None),
    )
    out_specs = P("row", "col", None, None)
    return jax.shard_map(body, mesh=mesh, in_specs=in_specs, out_specs=out_specs, check_vma=False)
```

time: 48.2 us -> 43.9 us (0.911)
  local copies, waits for them, and re-layouts: 2.26 us -> 0 us
  Pallas kernels: 45.8 us -> 43.7 us
    unnamed x1 -> x0, local copies, waits for them, and re-layouts: 2.26 us -> none
    pallas_call x1 -> x2, Pallas kernels: 45.8 us -> 43.7 us  [the longest x1 40.9 us: body(): pl.pallas_call(kernel, out_shape=jax.ShapeDtypeStruct((rhs, rank), f32),...]
where the time goes in v2:
time: 43.9 us; the launch traced here: 43.7 us
  Pallas kernels  43.7 us (100%)
    pallas_call x1, Pallas kernels, body(): pl.pallas_call(kernel, out_shape=jax.ShapeDtypeStruct((rhs, rank), f32),...  40.9 us
    pallas_call x1, Pallas kernels, body(): pl.pallas_call(expand, grid=(rhs // wide,), out_shape=jax.ShapeDtypeStruc...  2.78 us

profile of v2, /device:TPU:0, one launch (start us, length us, event | category | flops | bytes accessed | tf_op | source)
XLA Modules:
  0.0 43.7 jit_solution(10561884604751928815)
XLA Ops:
  0.0 40.9 %shard_map.46.last = f32[512,256]{1,0:T(8,128)} custom-call(f32[512,512]{1,0:T(8,128)} %bitcast.6, f32[512,256]{1,0:T(8,128)} %bitcast.8, f32[4,256,512]{2,1,0:T(8,128)} %bitcast.5), custom_call_target="tpu_custom_call" | custom-call | tf_op jit(solution)/shard_map/pallas_call | solution.py:156
  41.0 2.8 %shard_map.47 = f32[512,512]{1,0:T(8,128)} custom-call(f32[512,256]{1,0:T(8,128)} %shard_map.46.last, f32[512,256]{1,0:T(8,128)} %bitcast.7), custom_call_target="tpu_custom_call" | custom-call | tf_op jit(solution)/shard_map/pallas_call | solution.py:178
